TPU v7x, 32 devices: a whole 2x2x4 slice. The times are simulated.
32 devices in a mesh: bits: 16 (over z, y, x), docs: 2 (over core).
Axes of the slice: x: 2, y: 2, z: 4, core: 2. Of those that a mesh axis runs over, the one named last changes fastest.
Arguments:
- positions: int32 [1024, 4096], P(('bits', 'docs')), may hold values from 0 to 4095
- element_weights: float32 [1024, 1024], P(('bits', 'docs')), may hold values from 0.25 to 4
- set_sizes: int32 [1024], P(('bits', 'docs')), may hold values from 256 to 1024, as said below
- bit_weights: bfloat16 [4096], replicated, may hold values from 0.25 to 4
- candidates: int32 [2, 16, 16], P('docs'), may hold values from 0 to 63, as said below
Outputs:
- scores: float32 [2, 16, 128, 64], P('docs', 'bits')
Inputs may be any that keep to these rules, and one draw needn't show every extreme that they name: `set_sizes`: one document in every draw has exactly 1024 elements. `candidates`: the 16 row tiles named for one block are distinct. `positions`: entries of a row beyond its first 4 * set_sizes are not part of the filter.
All inputs are finite; a program needn't handle non-finite values.
Results may differ from a plain program's by a relative error of at most 0.0012.
Values may be sent and summed in bfloat16 or wider, within the bound.
A program may use at most 64 MiB of HBM per device.

v0:
```python
import functools
import math

import jax
import jax.numpy as jnp
from jax import lax
from jax.experimental import pallas as pl
from jax.experimental.pallas import tpu as pltpu
from jax.sharding import PartitionSpec as P

FILTER_BITS = 4096
HASHES = 4
TILE = 8
LANES = 128
CHUNK = 512
UNROLL = 12
PARTS = 2
MESH = pl.DeviceIdType.MESH


def build_filter(positions, element_weights, set_sizes):
    doc_count, slot_count = positions.shape
    elem_count = element_weights.shape[1]
    low_cells = 64
    high_cells = FILTER_BITS // low_cells
    slot_index = jnp.arange(slot_count, dtype=jnp.int32)
    usable = slot_index[None, :] < HASHES * set_sizes[:, None]
    spread = jnp.broadcast_to(element_weights[:, :, None], (doc_count, elem_count, HASHES)).reshape(
        doc_count, slot_count
    )
    slot_weights = jnp.where(usable, spread, 0.0)
    upper = slot_weights.astype(jnp.bfloat16)
    remain = slot_weights - upper.astype(jnp.float32)
    middle = remain.astype(jnp.bfloat16)
    lower = (remain - middle.astype(jnp.float32)).astype(jnp.bfloat16)
    weight_parts = jnp.stack([upper, middle, lower], axis=1)
    high_index = positions // low_cells
    low_index = positions - high_index * low_cells
    group = math.gcd(doc_count, 8)

    def one_group(inputs):
        part_block, high_block, low_block = inputs
        high_onehot = (high_block[:, :, None] == jnp.arange(high_cells, dtype=jnp.int32)).astype(
            jnp.bfloat16
        )
        low_onehot = (low_block[:, :, None] == jnp.arange(low_cells, dtype=jnp.int32)).astype(
            jnp.bfloat16
        )
        left = part_block[:, :, :, None] * high_onehot[:, None, :, :]
        summed = jnp.einsum("dcph,dpl->dhl", left, low_onehot, preferred_element_type=jnp.float32)
        return summed.reshape(group, FILTER_BITS)

    grouped = lax.map(
        one_group,
        (
            weight_parts.reshape(doc_count // group, group, 3, slot_count),
            high_index.reshape(doc_count // group, group, slot_count),
            low_index.reshape(doc_count // group, group, slot_count),
        ),
    )
    return grouped.reshape(doc_count, FILTER_BITS).astype(jnp.bfloat16)


def weighted_pop(cells, weights):
    weighted = cells * weights
    return jnp.sum(weighted.astype(jnp.float32) * cells.astype(jnp.float32), axis=1)


def estimate(shared, pop_rows, pop_cols, size_rows, size_cols):
    union_weight = pop_rows[:, None] + pop_cols[None, :] - shared
    ratio = shared / union_weight
    smaller = jnp.minimum(size_rows[:, None], size_cols[None, :])
    return ratio * (size_rows[:, None] + size_cols[None, :]) / ((1.0 + ratio) * smaller)


def pick_tiles(slice_cells, tile_choice, row_group, groups, row_half):
    width = slice_cells.shape[1]
    row_tiles = row_half // TILE
    tiles = slice_cells.reshape(groups, row_tiles, TILE * width)
    own_tiles = lax.dynamic_index_in_dim(tiles, row_group, 0, keepdims=False)
    onehot = (tile_choice[:, :, None] == jnp.arange(row_tiles, dtype=jnp.int32)).astype(
        jnp.bfloat16
    )
    picked = jnp.einsum("jcr,rw->jcw", onehot, own_tiles, preferred_element_type=jnp.float32)
    return picked.astype(jnp.bfloat16).reshape(
        tile_choice.shape[0], tile_choice.shape[1] * TILE, width
    )


def body(positions, element_weights, set_sizes, bit_weights, candidates):
    col_index = lax.axis_index("bits")
    row_group = lax.axis_index("docs")
    blocks = lax.axis_size("bits")
    groups = lax.axis_size("docs")
    doc_total = positions.shape[0] * blocks * groups
    row_half = doc_total // groups
    col_width = doc_total // blocks
    slot_count = candidates.shape[2] * TILE
    tile_offsets = jnp.arange(TILE, dtype=jnp.int32)
    own_cells = build_filter(positions, element_weights, set_sizes)
    local_pop = weighted_pop(own_cells, bit_weights)
    every_pop, size_float = (
        lax.all_gather(local_pop, ("bits", "docs"), axis=0, tiled=True),
        lax.all_gather(set_sizes.astype(jnp.float32), ("bits", "docs"), axis=0, tiled=True),
    )
    pair_cells = lax.all_gather(own_cells, "docs", axis=0, tiled=True)
    slice_cells = lax.all_to_all(pair_cells, "bits", split_axis=1, concat_axis=0, tiled=True)
    tile_rows = row_group * row_half + (candidates[0][:, :, None] * TILE + tile_offsets).reshape(
        blocks, slot_count
    )
    picked_cells = pick_tiles(slice_cells, candidates[0], row_group, groups, row_half)
    row_cells = lax.all_to_all(picked_cells, "bits", split_axis=0, concat_axis=2, tiled=True)[0]
    shared = lax.dot_general(
        row_cells * bit_weights,
        pair_cells,
        (((1,), (1,)), ((), ())),
        preferred_element_type=jnp.float32,
    )
    row_docs = lax.dynamic_index_in_dim(tile_rows, col_index, 0, keepdims=False)
    pop_rows = every_pop[row_docs]
    pop_cols = lax.dynamic_slice_in_dim(every_pop, col_index * col_width, col_width, 0)
    size_rows = size_float[row_docs]
    size_cols = lax.dynamic_slice_in_dim(size_float, col_index * col_width, col_width, 0)
    scores = estimate(shared, pop_rows, pop_cols, size_rows, size_cols)
    return scores.reshape(1, 1, slot_count, col_width)


NT = (((1,), (1,)), ((), ()))


def filter_kernel(sizes_ref, pos_ref, elem_ref, bw_ref, cells_ref, stats_ref, spread, acc, rows):
    docs, slots = pos_ref.shape
    elems = elem_ref.shape[1]
    highs = FILTER_BITS // LANES
    lane = lax.broadcasted_iota(jnp.int32, (docs, LANES), 1)
    sub = lax.broadcasted_iota(jnp.int32, (docs, LANES), 0)
    size_of = jnp.zeros((docs, LANES), jnp.int32)
    total = jnp.int32(0)
    for d in range(docs):
        size = sizes_ref[d]
        size_of = jnp.where(sub == d, size, size_of)
        total = total + (HASHES * size + CHUNK - 1) // CHUNK
    width = 2 * LANES
    wide = (lax.broadcasted_iota(jnp.int32, (width, HASHES * width), 1) // HASHES
            == lax.broadcasted_iota(jnp.int32, (width, HASHES * width), 0))
    wide = jnp.where(wide, 1.0, 0.0).astype(jnp.bfloat16)
    size_wide = jnp.concatenate([size_of] * (width // LANES), axis=1)
    lane_wide = lax.broadcasted_iota(jnp.int32, (docs, width), 1)
    for q in range(elems // width):
        value = elem_ref[:, q * width:(q + 1) * width]
        value = jnp.where(lane_wide + q * width < size_wide, value, 0.0)
        upper = value.astype(jnp.bfloat16)
        lower = (value - upper.astype(jnp.float32)).astype(jnp.bfloat16)
        for p, part in enumerate((upper, lower)):
            spread[p, :, q * HASHES * width:(q + 1) * HASHES * width] = jnp.dot(
                part, wide, preferred_element_type=jnp.float32)

    @pl.loop(0, docs + 1)
    def _(d):
        acc[d] = jnp.zeros(acc.shape[1:], jnp.float32)

    low_iota = lax.broadcasted_iota(jnp.int32, (LANES, CHUNK), 0)
    high_iota = lax.broadcasted_iota(jnp.int32, (highs, CHUNK), 0)

    def group(_, carry):
        d, c = carry
        for _ in range(UNROLL):
            row = jnp.minimum(d, docs - 1)
            at = pl.ds(pl.multiple_of(c * CHUNK, CHUNK), CHUNK)
            pos = pos_ref[pl.ds(row, 1), at]
            high, low = lax.shift_right_logical(pos, 7), lax.bitwise_and(pos, LANES - 1)
            left = jnp.where(low == low_iota, 1.0, 0.0).astype(jnp.bfloat16)
            hit = high == high_iota
            right = jnp.concatenate(
                [jnp.where(hit, spread[p, pl.ds(row, 1), at], 0.0) for p in range(PARTS)],
                axis=0).astype(jnp.bfloat16)
            acc[d] = acc[d] + lax.dot_general(left, right, NT, preferred_element_type=jnp.float32)
            more = (c + 1) * CHUNK < HASHES * sizes_ref[row]
            c = jnp.where(more, c + 1, 0)
            d = jnp.where(more, d, jnp.minimum(d + 1, docs))
            c = jnp.where(d == docs, 0, c)
        return d, c

    lax.fori_loop(0, (total + UNROLL - 1) // UNROLL, group, (jnp.int32(0), jnp.int32(0)))

    @pl.loop(0, docs)
    def _(d):
        both = acc[d].T
        rows[pl.ds(d, highs, stride=docs), :] = both[:highs] + both[highs:]

    span = cells_ref.shape[2]
    pop = jnp.zeros((docs, LANES), jnp.float32)
    for h in range(highs):
        cells = rows[h * docs:(h + 1) * docs, :].astype(jnp.bfloat16)
        cells_ref[h * LANES // span, :, h * LANES % span:h * LANES % span + LANES] = cells
        full = cells.astype(jnp.float32)
        weight = bw_ref[h * LANES:(h + 1) * LANES].astype(jnp.float32).reshape(1, LANES)
        pop = pop + (full * weight).astype(jnp.bfloat16).astype(jnp.float32) * full
    pop = jnp.sum(pop, axis=1, keepdims=True)
    both = jnp.where(lane == sub, pop, 0.0)
    both = jnp.where(lane == sub + docs, size_of.astype(jnp.float32), both)
    stats_ref[...] = jnp.sum(both, axis=0, keepdims=True)


def make_filter(positions, element_weights, set_sizes, weights, pieces):
    docs, slots = positions.shape
    vmem = pl.BlockSpec(memory_space=pltpu.VMEM)
    highs = FILTER_BITS // LANES
    return pl.pallas_call(
        filter_kernel,
        out_shape=(
            jax.ShapeDtypeStruct((pieces, docs, FILTER_BITS // pieces), jnp.bfloat16),
            jax.ShapeDtypeStruct((1, LANES), jnp.float32),
        ),
        in_specs=[pl.BlockSpec(memory_space=pltpu.SMEM), vmem, vmem, vmem],
        out_specs=(vmem, vmem),
        scratch_shapes=[
            pltpu.VMEM((PARTS, docs, slots), jnp.float32),
            pltpu.VMEM((docs + 1, LANES, PARTS * highs), jnp.float32),
            pltpu.VMEM((highs * docs, LANES), jnp.float32),
        ],
    )(set_sizes, positions, element_weights, weights)


def score_kernel(blocks, groups, cand_ref, cells_ref, stats_ref, bw_ref, out_ref,
                 slab, stat, weighted, part, inbox,
                 send1, recv1, send1s, recv1s, send2, recv2, send2s, recv2s, send3, recv3):
    col, grp = lax.axis_index("bits"), lax.axis_index("docs")
    docs, span = cells_ref.shape[1:]
    picks = cand_ref.shape[2]
    owners = blocks * groups
    row_half = docs * owners // groups
    width = docs * groups
    me = col * groups + grp

    barrier = pltpu.get_barrier_semaphore()
    for k in range(1, blocks):
        pl.semaphore_signal(barrier, inc=1, device_id=(lax.rem(col + k, blocks), grp), device_id_type=MESH)
    for k in range(1, groups):
        pl.semaphore_signal(barrier, inc=1, device_id=(col, lax.rem(grp + k, groups)), device_id_type=MESH)
    pl.semaphore_wait(barrier, blocks + groups - 2)

    def remote(src, dst, send, recv, device):
        return pltpu.make_async_remote_copy(
            src_ref=src, dst_ref=dst, send_sem=send, recv_sem=recv, device_id=device, device_id_type=MESH)

    order = sorted(range(1, blocks), key=lambda k: -min(k, blocks - k))
    first, stats = {}, {}
    for k in order:
        to = lax.rem(col + k, blocks)
        first[k] = remote(cells_ref.at[to], slab.at[me], send1.at[k], recv1.at[k], (to, grp))
        stats[k] = remote(stats_ref.at[0], stat.at[me], send1s.at[k], recv1s.at[k], (to, grp))
        first[k].start()
        stats[k].start()
    slab[me] = cells_ref[col]
    stat[me] = stats_ref[0]

    second = []
    other = lax.rem(grp + 1, groups)
    for k in [0] + order[::-1]:
        if k:
            first[k].wait_recv()
            stats[k].wait_recv()
        came = lax.rem(col - k + blocks, blocks)
        slot = came * groups + grp
        source = cells_ref.at[col] if k == 0 else slab.at[slot]
        source_s = stats_ref.at[0] if k == 0 else stat.at[slot]
        pair = (remote(source, slab.at[slot], send2.at[k], recv2.at[k], (col, other)),
                remote(source_s, stat.at[slot], send2s.at[k], recv2s.at[k], (col, other)))
        for copy in pair:
            copy.start()
        second.extend(pair)
    for copy in second:
        copy.wait_recv()

    bw = bw_ref[pl.ds(pl.multiple_of(col * span, span), span)].astype(jnp.float32).reshape(1, span)
    near = docs // TILE
    for o in range(owners // groups):
        value = slab[grp * (owners // groups) + o].astype(jnp.float32) * bw
        value = value.astype(jnp.bfloat16).astype(jnp.float32)
        for t in range(near):
            weighted[o * near + t] = value[t * TILE:(t + 1) * TILE]

    third = []
    for k in order + [0]:
        block = lax.rem(col + k, blocks)
        tiles = [weighted[cand_ref[0, block, c]] for c in range(picks)]
        lines = jnp.concatenate(tiles, axis=0).astype(jnp.bfloat16)
        columns = jnp.concatenate([slab[block * groups + o] for o in range(groups)], axis=0)
        shared = lax.dot_general(columns, lines, NT, preferred_element_type=jnp.float32)
        if k:
            part[k] = shared.astype(part.dtype)
            copy = remote(part.at[k], inbox.at[k], send3.at[k], recv3.at[k], (block, grp))
            copy.start()
            third.append((k, copy))

    eight = lax.broadcasted_iota(jnp.int32, (TILE, LANES), 0)
    lanes = lax.broadcasted_iota(jnp.int32, (TILE, LANES), 1)
    pop_rows = jnp.zeros((TILE, LANES), jnp.float32)
    size_rows = jnp.zeros((TILE, LANES), jnp.float32)
    for c in range(picks):
        tile = cand_ref[0, col, c]
        line = stat[grp * (owners // groups) + lax.div(tile, near)]
        spot = lanes - lax.rem(tile, near) * TILE - eight
        pop = jnp.sum(jnp.where(spot == 0, line, 0.0), axis=1, keepdims=True)
        size = jnp.sum(jnp.where(spot == docs, line, 0.0), axis=1, keepdims=True)
        here = lanes == eight + c * TILE
        pop_rows = jnp.where(here, pop, pop_rows)
        size_rows = jnp.where(here, size, size_rows)
    pop_rows = jnp.sum(pop_rows, axis=0, keepdims=True)
    size_rows = jnp.sum(size_rows, axis=0, keepdims=True)
    sub = lax.broadcasted_iota(jnp.int32, (docs, LANES), 0)
    lane = lax.broadcasted_iota(jnp.int32, (docs, LANES), 1)
    mine = [stat[col * groups + o] for o in range(groups)]
    pop_cols = jnp.concatenate(
        [jnp.sum(jnp.where(lane == sub, line, 0.0), axis=1, keepdims=True) for line in mine], axis=0)
    size_cols = jnp.concatenate(
        [jnp.sum(jnp.where(lane == sub + docs, line, 0.0), axis=1, keepdims=True) for line in mine], axis=0)

    for k, copy in third[::-1]:
        copy.wait_recv()
        shared = shared + inbox[k].astype(jnp.float32)
    ratio = shared / (pop_rows + pop_cols - shared)
    out_ref[...] = ratio * (size_rows + size_cols) / ((1.0 + ratio) * jnp.minimum(size_rows, size_cols))
    for copy in [*first.values(), *stats.values(), *second] + [copy for _, copy in third]:
        copy.wait_send()


def fast_body(blocks, groups, positions, element_weights, set_sizes, bit_weights, candidates):
    docs = positions.shape[0]
    weights = bit_weights
    cells, stats = make_filter(positions, element_weights, set_sizes, weights, blocks)
    span = cells.shape[2]
    width, rows = docs * groups, candidates.shape[2] * TILE
    vmem = pl.BlockSpec(memory_space=pltpu.VMEM)
    sems = lambda: pltpu.SemaphoreType.DMA((blocks,))
    scores = pl.pallas_call(
        functools.partial(score_kernel, blocks, groups),
        out_shape=jax.ShapeDtypeStruct((width, rows), jnp.float32),
        in_specs=[pl.BlockSpec(memory_space=pltpu.SMEM), vmem, vmem, vmem],
        out_specs=vmem,
        scratch_shapes=[
            pltpu.VMEM((blocks * groups, docs, span), jnp.bfloat16),
            pltpu.VMEM((blocks * groups, 1, LANES), jnp.float32),
            pltpu.VMEM((docs * blocks // TILE, TILE, span), jnp.float32),
            pltpu.VMEM((blocks, width, rows), jnp.bfloat16),
            pltpu.VMEM((blocks, width, rows), jnp.bfloat16),
        ] + [sems() for _ in range(10)],
        compiler_params=pltpu.CompilerParams(collective_id=0, has_side_effects=True),
    )(candidates, cells, stats.reshape(1, 1, LANES), weights)
    return scores.T.reshape(1, 1, rows, width)


def solution(mesh):
    blocks, groups = mesh.shape["bits"], mesh.shape["docs"]
    fits = groups == 2 and FILTER_BITS % (blocks * LANES) == 0
    chosen = functools.partial(fast_body, blocks, groups) if fits else body
    return jax.shard_map(
        chosen,
        mesh=mesh,
        in_specs=(
            P(("bits", "docs"), None),
            P(("bits", "docs"), None),
            P(("bits", "docs")),
            P(),
            P("docs", None, None),
        ),
        out_specs=P("docs", "bits", None, None),
        check_vma=False,
    )
```

profile of v0, /device:TPU:0, one launch (start us, length us, event | category | flops | bytes accessed | tf_op | source)
XLA Modules:
  0.0 41.2 jit_solution(4613038344776958270)
XLA Ops:
  0.0 13.2 %shard_map.55 = (bf16[16,32,256]{2,1,0:T(8,128)(2,1)}, f32[1,128]{1,0:T(1,128)}) custom-call(s32[32]{0:T(128)} %sizes_ref.1, s32[32,4096]{1,0:T(8,128)} %pos_ref.1, f32[32,1024]{1,0:T(8,128)} %elem_ref.1, bf16[4096]{0:T(1024)(128)(2,1)} %bw_ref.3), custom_call_target="tpu_custom_call" | custom-call | tf_op jit(solution)/shard_map/pallas_call | solution.py:209
  13.2 26.6 %shard_map.56 = f32[64,128]{1,0:T(8,128)} custom-call(s32[1,16,16]{2,1,0:T(8,128)} %cand_ref.1, bf16[16,32,256]{2,1,0:T(8,128)(2,1)} %get-tuple-element.7.cells_ref, f32[1,1,128]{2,1,0:T(1,128)} %bitcast.5, bf16[4096]{0:T(1024)(128)(2,1)} %bw_ref.3), custom_call_target="tpu_custom_call" | custom-call | tf_op jit(solution)/shard_map/pallas_call | solution.py:337
  39.8 1.4 %copy.7 = f32[1,1,128,64]{2,3,1,0:T(8,128)} copy(f32[1,1,128,64]{2,3,1,0:T(8,128)} %bitcast.4) | data formatting | bytes 65536
where the time goes:
time: 41.4 us; the launch traced here: 41.2 us
  Pallas kernels  39.8 us (96%)
  local copies, waits for them, and re-layouts  1.38 us (3%)
    pallas_call x1, Pallas kernels, fast_body(): pl.pallas_call(functools.partial(score_kernel, blocks, groups), out_shape...  26.6 us
    pallas_call x1, Pallas kernels, make_filter(): pl.pallas_call(filter_kernel, out_shape=(jax.ShapeDtypeStruct((pieces, do...  13.2 us
    unnamed x1, local copies, waits for them, and re-layouts  1.38 us

commit v1 on v0

v1 whole, which is shorter than its diff:
```python
import functools
import math

import jax
import jax.numpy as jnp
from jax import lax
from jax.experimental import pallas as pl
from jax.experimental.pallas import tpu as pltpu
from jax.sharding import PartitionSpec as P

FILTER_BITS = 4096
HASHES = 4
TILE = 8
LANES = 128
CHUNK = 512
STEPS = (0, 127, 126, 3, 122, 6, 125, 8)
MESH = pl.DeviceIdType.MESH


def build_filter(positions, element_weights, set_sizes):
    doc_count, slot_count = positions.shape
    elem_count = element_weights.shape[1]
    low_cells = 64
    high_cells = FILTER_BITS // low_cells
    slot_index = jnp.arange(slot_count, dtype=jnp.int32)
    usable = slot_index[None, :] < HASHES * set_sizes[:, None]
    spread = jnp.broadcast_to(element_weights[:, :, None], (doc_count, elem_count, HASHES)).reshape(
        doc_count, slot_count
    )
    slot_weights = jnp.where(usable, spread, 0.0)
    upper = slot_weights.astype(jnp.bfloat16)
    remain = slot_weights - upper.astype(jnp.float32)
    middle = remain.astype(jnp.bfloat16)
    lower = (remain - middle.astype(jnp.float32)).astype(jnp.bfloat16)
    weight_parts = jnp.stack([upper, middle, lower], axis=1)
    high_index = positions // low_cells
    low_index = positions - high_index * low_cells
    group = math.gcd(doc_count, 8)

    def one_group(inputs):
        part_block, high_block, low_block = inputs
        high_onehot = (high_block[:, :, None] == jnp.arange(high_cells, dtype=jnp.int32)).astype(
            jnp.bfloat16
        )
        low_onehot = (low_block[:, :, None] == jnp.arange(low_cells, dtype=jnp.int32)).astype(
            jnp.bfloat16
        )
        left = part_block[:, :, :, None] * high_onehot[:, None, :, :]
        summed = jnp.einsum("dcph,dpl->dhl", left, low_onehot, preferred_element_type=jnp.float32)
        return summed.reshape(group, FILTER_BITS)

    grouped = lax.map(
        one_group,
        (
            weight_parts.reshape(doc_count // group, group, 3, slot_count),
            high_index.reshape(doc_count // group, group, slot_count),
            low_index.reshape(doc_count // group, group, slot_count),
        ),
    )
    return grouped.reshape(doc_count, FILTER_BITS).astype(jnp.bfloat16)


def weighted_pop(cells, weights):
    weighted = cells * weights
    return jnp.sum(weighted.astype(jnp.float32) * cells.astype(jnp.float32), axis=1)


def estimate(shared, pop_rows, pop_cols, size_rows, size_cols):
    union_weight = pop_rows[:, None] + pop_cols[None, :] - shared
    ratio = shared / union_weight
    smaller = jnp.minimum(size_rows[:, None], size_cols[None, :])
    return ratio * (size_rows[:, None] + size_cols[None, :]) / ((1.0 + ratio) * smaller)


def pick_tiles(slice_cells, tile_choice, row_group, groups, row_half):
    width = slice_cells.shape[1]
    row_tiles = row_half // TILE
    tiles = slice_cells.reshape(groups, row_tiles, TILE * width)
    own_tiles = lax.dynamic_index_in_dim(tiles, row_group, 0, keepdims=False)
    onehot = (tile_choice[:, :, None] == jnp.arange(row_tiles, dtype=jnp.int32)).astype(
        jnp.bfloat16
    )
    picked = jnp.einsum("jcr,rw->jcw", onehot, own_tiles, preferred_element_type=jnp.float32)
    return picked.astype(jnp.bfloat16).reshape(
        tile_choice.shape[0], tile_choice.shape[1] * TILE, width
    )


def body(positions, element_weights, set_sizes, bit_weights, candidates):
    col_index = lax.axis_index("bits")
    row_group = lax.axis_index("docs")
    blocks = lax.axis_size("bits")
    groups = lax.axis_size("docs")
    doc_total = positions.shape[0] * blocks * groups
    row_half = doc_total // groups
    col_width = doc_total // blocks
    slot_count = candidates.shape[2] * TILE
    tile_offsets = jnp.arange(TILE, dtype=jnp.int32)
    own_cells = build_filter(positions, element_weights, set_sizes)
    local_pop = weighted_pop(own_cells, bit_weights)
    every_pop, size_float = (
        lax.all_gather(local_pop, ("bits", "docs"), axis=0, tiled=True),
        lax.all_gather(set_sizes.astype(jnp.float32), ("bits", "docs"), axis=0, tiled=True),
    )
    pair_cells = lax.all_gather(own_cells, "docs", axis=0, tiled=True)
    slice_cells = lax.all_to_all(pair_cells, "bits", split_axis=1, concat_axis=0, tiled=True)
    tile_rows = row_group * row_half + (candidates[0][:, :, None] * TILE + tile_offsets).reshape(
        blocks, slot_count
    )
    picked_cells = pick_tiles(slice_cells, candidates[0], row_group, groups, row_half)
    row_cells = lax.all_to_all(picked_cells, "bits", split_axis=0, concat_axis=2, tiled=True)[0]
    shared = lax.dot_general(
        row_cells * bit_weights,
        pair_cells,
        (((1,), (1,)), ((), ())),
        preferred_element_type=jnp.float32,
    )
    row_docs = lax.dynamic_index_in_dim(tile_rows, col_index, 0, keepdims=False)
    pop_rows = every_pop[row_docs]
    pop_cols = lax.dynamic_slice_in_dim(every_pop, col_index * col_width, col_width, 0)
    size_rows = size_float[row_docs]
    size_cols = lax.dynamic_slice_in_dim(size_float, col_index * col_width, col_width, 0)
    scores = estimate(shared, pop_rows, pop_cols, size_rows, size_cols)
    return scores.reshape(1, 1, slot_count, col_width)


NT = (((1,), (1,)), ((), ()))


def two_factors(value):
    best_a = value.astype(jnp.bfloat16).astype(jnp.float32)
    best_b = jnp.ones_like(value)
    best_e = jnp.abs(best_a - value)
    for step in STEPS[1:]:
        b = 1.0 + step / 128.0
        a = (value * (1.0 / b)).astype(jnp.bfloat16).astype(jnp.float32)
        e = jnp.abs(a * b - value)
        better = e < best_e
        best_a = jnp.where(better, a, best_a)
        best_b = jnp.where(better, b, best_b)
        best_e = jnp.where(better, e, best_e)
    return best_a, best_b


def fused_kernel(blocks, groups, cand_ref, sizes_ref, pos_ref, elem_ref, bw_ref, out_ref,
                 high_s, low_s, a_s, b_s, rows, outbox, stat_own, slab, stat, weighted, part, inbox,
                 send1, recv1, send1s, recv1s, send2, recv2, send2s, recv2s, send3, recv3):
    col, grp = lax.axis_index("bits"), lax.axis_index("docs")
    docs, slots = pos_ref.shape
    elems = elem_ref.shape[1]
    span = slab.shape[3]
    picks = cand_ref.shape[2]
    owners = blocks * groups
    near = docs // TILE
    me = col * groups + grp
    other = lax.rem(grp + 1, groups)
    half = LANES // 2
    highs = FILTER_BITS // half
    lines = FILTER_BITS // LANES

    barrier = pltpu.get_barrier_semaphore()
    for k in range(1, blocks):
        pl.semaphore_signal(barrier, inc=1, device_id=(lax.rem(col + k, blocks), grp), device_id_type=MESH)
    for k in range(1, groups):
        pl.semaphore_signal(barrier, inc=1, device_id=(col, lax.rem(grp + k, groups)), device_id_type=MESH)

    lane = lax.broadcasted_iota(jnp.int32, (docs, LANES), 1)
    sub = lax.broadcasted_iota(jnp.int32, (docs, LANES), 0)
    size_of = jnp.zeros((docs, LANES), jnp.int32)
    for d in range(docs):
        size_of = jnp.where(sub == d, sizes_ref[d], size_of)
    width = 2 * LANES
    wide = (lax.broadcasted_iota(jnp.int32, (width, HASHES * width), 1) // HASHES
            == lax.broadcasted_iota(jnp.int32, (width, HASHES * width), 0))
    wide = jnp.where(wide, 1.0, 0.0).astype(jnp.bfloat16)
    size_wide = jnp.concatenate([size_of] * (width // LANES), axis=1)
    lane_wide = lax.broadcasted_iota(jnp.int32, (docs, width), 1)
    for q in range(elems // width):
        value = elem_ref[:, q * width:(q + 1) * width]
        value = jnp.where(lane_wide + q * width < size_wide, value, 0.0)
        for place, part_of in zip((a_s, b_s), two_factors(value)):
            place[:, q * HASHES * width:(q + 1) * HASHES * width] = jnp.dot(
                part_of.astype(jnp.bfloat16), wide, preferred_element_type=jnp.float32)
    for q in range(slots // CHUNK):
        at = slice(q * CHUNK, (q + 1) * CHUNK)
        pos = pos_ref[:, at]
        high_s[:, at] = lax.shift_right_logical(pos, 6).astype(jnp.float32)
        low_s[:, at] = lax.bitwise_and(pos, half - 1).astype(jnp.float32)

    index = lax.broadcasted_iota(jnp.int32, (highs, LANES), 0)
    high_at = 2 * lax.rem(index, lines) + lax.div(index, lines)
    high_at = jnp.concatenate([high_at.astype(jnp.float32).astype(jnp.bfloat16)] * (CHUNK // LANES), axis=1)
    low_at = jnp.concatenate([index.astype(jnp.float32).astype(jnp.bfloat16)] * (CHUNK // LANES), axis=1)
    zero = jnp.zeros((half, CHUNK), jnp.bfloat16)

    def spread_row(ref, row, at):
        line = jnp.broadcast_to(ref[pl.ds(row, 1), at], (16, CHUNK)).astype(jnp.bfloat16)
        return jnp.concatenate([line] * (half // 16), axis=0)

    def remote(src, dst, send, recv, device):
        return pltpu.make_async_remote_copy(
            src_ref=src, dst_ref=dst, send_sem=send, recv_sem=recv, device_id=device, device_id_type=MESH)

    order = sorted(range(1, blocks), key=lambda k: -min(k, blocks - k))

    def first(q, k):
        to = lax.rem(col + k, blocks)
        return remote(outbox.at[q, to], slab.at[q, me], send1.at[q, k], recv1.at[q, k], (to, grp))

    def second(q, k):
        slot = lax.rem(col - k + blocks, blocks) * groups + grp
        source = slab.at[q, slot] if k else outbox.at[q, col]
        return remote(source, slab.at[q, slot], send2.at[q, k], recv2.at[q, k], (col, other))

    def first_stat(k):
        to = lax.rem(col + k, blocks)
        return remote(stat_own, stat.at[me], send1s.at[k], recv1s.at[k], (to, grp))

    def second_stat(k):
        slot = lax.rem(col - k + blocks, blocks) * groups + grp
        source = stat.at[slot] if k else stat_own
        return remote(source, stat.at[slot], send2s.at[k], recv2s.at[k], (col, other))

    def hand_on(q):
        for k in order[::-1]:
            first(q, k).wait_recv()
            second(q, k).start()

    def one_group(q, pops):
        for r in range(TILE):
            d = q * TILE + r
            total = jnp.zeros((highs, half), jnp.float32)
            for c in range(slots // CHUNK):
                at = slice(c * CHUNK, (c + 1) * CHUNK)
                left = jnp.where(spread_row(high_s, d, at) == high_at, spread_row(a_s, d, at), zero)
                right = jnp.where(spread_row(low_s, d, at) == low_at, spread_row(b_s, d, at), zero)
                total = total + lax.dot_general(left, right, NT, preferred_element_type=jnp.float32)
            rows[pl.ds(r, lines, stride=TILE), :] = jnp.concatenate([total[:lines], total[lines:]], axis=1)
        pop = jnp.zeros((TILE, LANES), jnp.float32)
        for h in range(lines):
            cells = rows[h * TILE:(h + 1) * TILE, :].astype(jnp.bfloat16)
            outbox[q, h * LANES // span, :, h * LANES % span:h * LANES % span + LANES] = cells
            full = cells.astype(jnp.float32)
            weight = bw_ref[h * LANES:(h + 1) * LANES].astype(jnp.float32).reshape(1, LANES)
            pop = pop + (full * weight).astype(jnp.bfloat16).astype(jnp.float32) * full
        pop = jnp.sum(pop, axis=1, keepdims=True)
        spot = lane[:TILE] == sub[:TILE] + q * TILE
        pops = pops + jnp.sum(jnp.where(spot, pop, 0.0), axis=0, keepdims=True)

        @pl.when(q == 0)
        def _():
            pl.semaphore_wait(barrier, blocks + groups - 2)

        for k in order:
            first(q, k).start()
        second(q, 0).start()
        slab[q, me] = outbox[q, col]

        @pl.when(q >= 2)
        def _():
            hand_on(q - 2)

        return pops

    pops = lax.fori_loop(0, near, one_group, jnp.zeros((1, LANES), jnp.float32))
    sizes = jnp.sum(jnp.where(lane == sub + docs, size_of.astype(jnp.float32), 0.0), axis=0, keepdims=True)
    stat_own[...] = pops + sizes
    for k in order:
        first_stat(k).start()
    second_stat(0).start()
    stat[me] = stat_own[...]
    for q in range(max(near - 2, 0), near):
        hand_on(q)
    for k in order[::-1]:
        first_stat(k).wait_recv()
        second_stat(k).start()
    for k in [0] + order[::-1]:
        for q in range(near):
            second(q, k).wait_recv()
        second_stat(k).wait_recv()

    bw = bw_ref[pl.ds(pl.multiple_of(col * span, span), span)].astype(jnp.float32).reshape(1, span)
    for o in range(owners // groups):
        for q in range(near):
            value = slab[q, grp * (owners // groups) + o].astype(jnp.float32) * bw
            weighted[o * near + q] = value.astype(jnp.bfloat16).astype(jnp.float32)

    third = []
    for k in order + [0]:
        block = lax.rem(col + k, blocks)
        tiles = [weighted[cand_ref[0, block, c]] for c in range(picks)]
        lines_in = jnp.concatenate(tiles, axis=0).astype(jnp.bfloat16)
        columns = jnp.concatenate(
            [slab[q, block * groups + o] for o in range(groups) for q in range(near)], axis=0)
        shared = lax.dot_general(columns, lines_in, NT, preferred_element_type=jnp.float32)
        if k:
            part[k] = shared.astype(part.dtype)
            copy = remote(part.at[k], inbox.at[k], send3.at[k], recv3.at[k], (block, grp))
            copy.start()
            third.append((k, copy))

    eight = lax.broadcasted_iota(jnp.int32, (TILE, LANES), 0)
    lanes = lax.broadcasted_iota(jnp.int32, (TILE, LANES), 1)
    pop_rows = jnp.zeros((TILE, LANES), jnp.float32)
    size_rows = jnp.zeros((TILE, LANES), jnp.float32)
    for c in range(picks):
        tile = cand_ref[0, col, c]
        line = stat[grp * (owners // groups) + lax.div(tile, near)]
        spot = lanes - lax.rem(tile, near) * TILE - eight
        pop = jnp.sum(jnp.where(spot == 0, line, 0.0), axis=1, keepdims=True)
        size = jnp.sum(jnp.where(spot == docs, line, 0.0), axis=1, keepdims=True)
        here = lanes == eight + c * TILE
        pop_rows = jnp.where(here, pop, pop_rows)
        size_rows = jnp.where(here, size, size_rows)
    pop_rows = jnp.sum(pop_rows, axis=0, keepdims=True)
    size_rows = jnp.sum(size_rows, axis=0, keepdims=True)
    mine = [stat[col * groups + o] for o in range(groups)]
    pop_cols = jnp.concatenate(
        [jnp.sum(jnp.where(lane == sub, line, 0.0), axis=1, keepdims=True) for line in mine], axis=0)
    size_cols = jnp.concatenate(
        [jnp.sum(jnp.where(lane == sub + docs, line, 0.0), axis=1, keepdims=True) for line in mine], axis=0)

    for k, copy in third[::-1]:
        copy.wait_recv()
        shared = shared + inbox[k].astype(jnp.float32)
    ratio = shared / (pop_rows + pop_cols - shared)
    out_ref[...] = ratio * (size_rows + size_cols) / ((1.0 + ratio) * jnp.minimum(size_rows, size_cols))
    for k, copy in third:
        copy.wait_send()
    for k in [0] + order:
        for q in range(near):
            if k:
                first(q, k).wait_send()
            second(q, k).wait_send()
        if k:
            first_stat(k).wait_send()
        second_stat(k).wait_send()


def fast_body(blocks, groups, positions, element_weights, set_sizes, bit_weights, candidates):
    docs, slots = positions.shape
    span = FILTER_BITS // blocks
    owners, near = blocks * groups, docs // TILE
    width, rows = docs * groups, candidates.shape[2] * TILE
    vmem, smem = pl.BlockSpec(memory_space=pltpu.VMEM), pl.BlockSpec(memory_space=pltpu.SMEM)
    one = lambda: pltpu.SemaphoreType.DMA((blocks,))
    many = lambda: pltpu.SemaphoreType.DMA((near, blocks))
    scores = pl.pallas_call(
        functools.partial(fused_kernel, blocks, groups),
        out_shape=jax.ShapeDtypeStruct((width, rows), jnp.float32),
        in_specs=[smem, smem, vmem, vmem, vmem],
        out_specs=vmem,
        scratch_shapes=[pltpu.VMEM((docs, slots), jnp.float32)] * 4 + [
            pltpu.VMEM((FILTER_BITS // LANES * TILE, LANES), jnp.float32),
            pltpu.VMEM((near, blocks, TILE, span), jnp.bfloat16),
            pltpu.VMEM((1, LANES), jnp.float32),
            pltpu.VMEM((near, owners, TILE, span), jnp.bfloat16),
            pltpu.VMEM((owners, 1, LANES), jnp.float32),
            pltpu.VMEM((docs * blocks // TILE, TILE, span), jnp.float32),
            pltpu.VMEM((blocks, width, rows), jnp.bfloat16),
            pltpu.VMEM((blocks, width, rows), jnp.bfloat16),
        ] + [many(), many(), one(), one(), many(), many(), one(), one(), one(), one()],
        compiler_params=pltpu.CompilerParams(collective_id=0, has_side_effects=True),
    )(candidates, set_sizes, positions, element_weights, bit_weights)
    return scores.T.reshape(1, 1, rows, width)


def solution(mesh):
    blocks, groups = mesh.shape["bits"], mesh.shape["docs"]
    fits = groups == 2 and FILTER_BITS % (blocks * LANES) == 0
    chosen = functools.partial(fast_body, blocks, groups) if fits else body
    return jax.shard_map(
        chosen,
        mesh=mesh,
        in_specs=(
            P(("bits", "docs"), None),
            P(("bits", "docs"), None),
            P(("bits", "docs")),
            P(),
            P("docs", None, None),
        ),
        out_specs=P("docs", "bits", None, None),
        check_vma=False,
    )
```

time: 41.4 us -> 33.3 us (0.80)
  Pallas kernels: 39.8 us -> 31.7 us
    pallas_call x2 -> x1, Pallas kernels: 39.8 us -> 31.7 us  [fast_body(): pl.pallas_call(functools.partial(fused_kernel, blocks, groups), out_shape...]
where the time goes in v1:
time: 33.3 us; the launch traced here: 33.1 us
  Pallas kernels  31.7 us (95%)
  local copies, waits for them, and re-layouts  1.38 us (4%)
    pallas_call x1, Pallas kernels, fast_body(): pl.pallas_call(functools.partial(fused_kernel, blocks, groups), out_shape...  31.7 us
    unnamed x1, local copies, waits for them, and re-layouts  1.38 us

profile of v1, /device:TPU:0, one launch (start us, length us, event | category | flops | bytes accessed | tf_op | source)
XLA Modules:
  0.0 33.1 jit_solution(339979870814767435)
XLA Ops:
  0.0 31.7 %shard_map.55 = f32[64,128]{1,0:T(8,128)} custom-call(s32[1,16,16]{2,1,0:T(8,128)} %cand_ref.1, s32[32]{0:T(128)} %sizes_ref.1, s32[32,4096]{1,0:T(8,128)} %pos_ref.1, f32[32,1024]{1,0:T(8,128)} %elem_ref.1, bf16[4096]{0:T(1024)(128)(2,1)} %bw_ref.1), custom_call_target="tpu_custom_call" | custom-call | tf_op jit(solution)/shard_map/pallas_call | solution.py:348
  31.7 1.4 %copy.7 = f32[1,1,128,64]{2,3,1,0:T(8,128)} copy(f32[1,1,128,64]{2,3,1,0:T(8,128)} %bitcast.3) | data formatting | bytes 65536

commit v2 on v1

v2 whole, which is shorter than its diff:
```python
import functools
import math

import jax
import jax.numpy as jnp
from jax import lax
from jax.experimental import pallas as pl
from jax.experimental.pallas import tpu as pltpu
from jax.sharding import PartitionSpec as P

FILTER_BITS = 4096
HASHES = 4
TILE = 8
LANES = 128
CHUNK = 512
STEPS = (0, 127, 126, 3, 122, 6, 125, 8)
MESH = pl.DeviceIdType.MESH


def build_filter(positions, element_weights, set_sizes):
    doc_count, slot_count = positions.shape
    elem_count = element_weights.shape[1]
    low_cells = 64
    high_cells = FILTER_BITS // low_cells
    slot_index = jnp.arange(slot_count, dtype=jnp.int32)
    usable = slot_index[None, :] < HASHES * set_sizes[:, None]
    spread = jnp.broadcast_to(element_weights[:, :, None], (doc_count, elem_count, HASHES)).reshape(
        doc_count, slot_count
    )
    slot_weights = jnp.where(usable, spread, 0.0)
    upper = slot_weights.astype(jnp.bfloat16)
    remain = slot_weights - upper.astype(jnp.float32)
    middle = remain.astype(jnp.bfloat16)
    lower = (remain - middle.astype(jnp.float32)).astype(jnp.bfloat16)
    weight_parts = jnp.stack([upper, middle, lower], axis=1)
    high_index = positions // low_cells
    low_index = positions - high_index * low_cells
    group = math.gcd(doc_count, 8)

    def one_group(inputs):
        part_block, high_block, low_block = inputs
        high_onehot = (high_block[:, :, None] == jnp.arange(high_cells, dtype=jnp.int32)).astype(
            jnp.bfloat16
        )
        low_onehot = (low_block[:, :, None] == jnp.arange(low_cells, dtype=jnp.int32)).astype(
            jnp.bfloat16
        )
        left = part_block[:, :, :, None] * high_onehot[:, None, :, :]
        summed = jnp.einsum("dcph,dpl->dhl", left, low_onehot, preferred_element_type=jnp.float32)
        return summed.reshape(group, FILTER_BITS)

    grouped = lax.map(
        one_group,
        (
            weight_parts.reshape(doc_count // group, group, 3, slot_count),
            high_index.reshape(doc_count // group, group, slot_count),
            low_index.reshape(doc_count // group, group, slot_count),
        ),
    )
    return grouped.reshape(doc_count, FILTER_BITS).astype(jnp.bfloat16)


def weighted_pop(cells, weights):
    weighted = cells * weights
    return jnp.sum(weighted.astype(jnp.float32) * cells.astype(jnp.float32), axis=1)


def estimate(shared, pop_rows, pop_cols, size_rows, size_cols):
    union_weight = pop_rows[:, None] + pop_cols[None, :] - shared
    ratio = shared / union_weight
    smaller = jnp.minimum(size_rows[:, None], size_cols[None, :])
    return ratio * (size_rows[:, None] + size_cols[None, :]) / ((1.0 + ratio) * smaller)


def pick_tiles(slice_cells, tile_choice, row_group, groups, row_half):
    width = slice_cells.shape[1]
    row_tiles = row_half // TILE
    tiles = slice_cells.reshape(groups, row_tiles, TILE * width)
    own_tiles = lax.dynamic_index_in_dim(tiles, row_group, 0, keepdims=False)
    onehot = (tile_choice[:, :, None] == jnp.arange(row_tiles, dtype=jnp.int32)).astype(
        jnp.bfloat16
    )
    picked = jnp.einsum("jcr,rw->jcw", onehot, own_tiles, preferred_element_type=jnp.float32)
    return picked.astype(jnp.bfloat16).reshape(
        tile_choice.shape[0], tile_choice.shape[1] * TILE, width
    )


def body(positions, element_weights, set_sizes, bit_weights, candidates):
    col_index = lax.axis_index("bits")
    row_group = lax.axis_index("docs")
    blocks = lax.axis_size("bits")
    groups = lax.axis_size("docs")
    doc_total = positions.shape[0] * blocks * groups
    row_half = doc_total // groups
    col_width = doc_total // blocks
    slot_count = candidates.shape[2] * TILE
    tile_offsets = jnp.arange(TILE, dtype=jnp.int32)
    own_cells = build_filter(positions, element_weights, set_sizes)
    local_pop = weighted_pop(own_cells, bit_weights)
    every_pop, size_float = (
        lax.all_gather(local_pop, ("bits", "docs"), axis=0, tiled=True),
        lax.all_gather(set_sizes.astype(jnp.float32), ("bits", "docs"), axis=0, tiled=True),
    )
    pair_cells = lax.all_gather(own_cells, "docs", axis=0, tiled=True)
    slice_cells = lax.all_to_all(pair_cells, "bits", split_axis=1, concat_axis=0, tiled=True)
    tile_rows = row_group * row_half + (candidates[0][:, :, None] * TILE + tile_offsets).reshape(
        blocks, slot_count
    )
    picked_cells = pick_tiles(slice_cells, candidates[0], row_group, groups, row_half)
    row_cells = lax.all_to_all(picked_cells, "bits", split_axis=0, concat_axis=2, tiled=True)[0]
    shared = lax.dot_general(
        row_cells * bit_weights,
        pair_cells,
        (((1,), (1,)), ((), ())),
        preferred_element_type=jnp.float32,
    )
    row_docs = lax.dynamic_index_in_dim(tile_rows, col_index, 0, keepdims=False)
    pop_rows = every_pop[row_docs]
    pop_cols = lax.dynamic_slice_in_dim(every_pop, col_index * col_width, col_width, 0)
    size_rows = size_float[row_docs]
    size_cols = lax.dynamic_slice_in_dim(size_float, col_index * col_width, col_width, 0)
    scores = estimate(shared, pop_rows, pop_cols, size_rows, size_cols)
    return scores.reshape(1, 1, slot_count, col_width)


NT = (((1,), (1,)), ((), ()))


def two_factors(value):
    best_a = value.astype(jnp.bfloat16).astype(jnp.float32)
    best_b = jnp.ones_like(value)
    best_e = jnp.abs(best_a - value)
    for step in STEPS[1:]:
        b = 1.0 + step / 128.0
        a = (value * (1.0 / b)).astype(jnp.bfloat16).astype(jnp.float32)
        e = jnp.abs(a * b - value)
        better = e < best_e
        best_a = jnp.where(better, a, best_a)
        best_b = jnp.where(better, b, best_b)
        best_e = jnp.where(better, e, best_e)
    return best_a, best_b


def fused_kernel(blocks, groups, cand_ref, sizes_ref, pos_ref, elem_ref, bw_ref, out_ref,
                 spread, rows, outbox, stat_own, slab, stat, weighted, part, inbox,
                 send1, recv1, send1s, recv1s, send2, recv2, send2s, recv2s, send3, recv3):
    col, grp = lax.axis_index("bits"), lax.axis_index("docs")
    docs, slots = pos_ref.shape
    elems = elem_ref.shape[1]
    span = slab.shape[4]
    picks = cand_ref.shape[2]
    near = docs // TILE
    other = 1 - grp
    half = LANES // 2
    highs = FILTER_BITS // half
    lines = FILTER_BITS // LANES
    peers = blocks - 1

    def shifted(k):
        return lax.bitwise_and(col + k, blocks - 1)

    barrier = pltpu.get_barrier_semaphore()
    for k in range(1, blocks):
        pl.semaphore_signal(barrier, inc=1, device_id=(shifted(k), grp), device_id_type=MESH)
    pl.semaphore_signal(barrier, inc=1, device_id=(col, other), device_id_type=MESH)

    lane = lax.broadcasted_iota(jnp.int32, (docs, LANES), 1)
    sub = lax.broadcasted_iota(jnp.int32, (docs, LANES), 0)
    lane8, sub8 = lane[:TILE], sub[:TILE]
    takes = [lax.div(lane8, HASHES) + j * (LANES // HASHES) for j in range(HASHES)]

    def prepare(q):
        size_of = jnp.zeros((TILE, LANES), jnp.int32)
        for r in range(TILE):
            size_of = jnp.where(sub8 == r, sizes_ref[q * TILE + r], size_of)
        docs_at = slice(q * TILE, (q + 1) * TILE)
        for e in range(elems // LANES):
            value = elem_ref[docs_at, e * LANES:(e + 1) * LANES]
            value = jnp.where(lane8 + e * LANES < size_of, value, 0.0)
            for p, factor in enumerate(two_factors(value)):
                for j, take in enumerate(takes):
                    at = (e * HASHES + j) * LANES
                    spread[q][2 + p, :, at:at + LANES] = jnp.take_along_axis(factor, take, axis=1)
        for e in range(slots // LANES):
            at = slice(e * LANES, (e + 1) * LANES)
            pos = pos_ref[docs_at, at]
            spread[q][0, :, at] = lax.shift_right_logical(pos, 6).astype(jnp.float32)
            spread[q][1, :, at] = lax.bitwise_and(pos, half - 1).astype(jnp.float32)
        return size_of

    index = lax.broadcasted_iota(jnp.int32, (highs, LANES), 0)
    high_at = 2 * lax.rem(index, lines) + lax.div(index, lines)
    high_at = jnp.concatenate([high_at.astype(jnp.float32).astype(jnp.bfloat16)] * (CHUNK // LANES), axis=1)
    low_at = jnp.concatenate([index.astype(jnp.float32).astype(jnp.bfloat16)] * (CHUNK // LANES), axis=1)
    zero = jnp.zeros((half, CHUNK), jnp.bfloat16)

    def remote(src, dst, send, recv, device):
        return pltpu.make_async_remote_copy(
            src_ref=src, dst_ref=dst, send_sem=send, recv_sem=recv, device_id=device, device_id_type=MESH)

    order = sorted(range(1, blocks), key=lambda k: -min(k, blocks - k))

    def build(q):
        for r in range(TILE):
            total = jnp.zeros((highs, half), jnp.float32)
            for c in range(slots // CHUNK):
                at = slice(c * CHUNK, (c + 1) * CHUNK)

                def row(which):
                    line = jnp.broadcast_to(spread[q][which, r:r + 1, at], (16, CHUNK)).astype(jnp.bfloat16)
                    return jnp.concatenate([line] * (half // 16), axis=0)

                left = jnp.where(row(0) == high_at, row(2), zero)
                right = jnp.where(row(1) == low_at, row(3), zero)
                total = total + lax.dot_general(left, right, NT, preferred_element_type=jnp.float32)
            rows[q][pl.ds(r, lines, stride=TILE), :] = jnp.concatenate([total[:lines], total[lines:]], axis=1)
        pop = jnp.zeros((TILE, LANES), jnp.float32)
        for h in range(lines):
            cells = rows[q][h * TILE:(h + 1) * TILE, :].astype(jnp.bfloat16)
            outbox[q, h * LANES // span, :, h * LANES % span:h * LANES % span + LANES] = cells
            full = cells.astype(jnp.float32)
            weight = bw_ref[h * LANES:(h + 1) * LANES].astype(jnp.float32).reshape(1, LANES)
            pop = pop + (full * weight).astype(jnp.bfloat16).astype(jnp.float32) * full
        pop = jnp.sum(pop, axis=1, keepdims=True)
        return jnp.sum(jnp.where(lane8 == sub8 + q * TILE, pop, 0.0), axis=0, keepdims=True)

    last = near - 1
    line = jnp.zeros((1, LANES), jnp.float32)
    size_of = prepare(0)
    for q in range(near):
        size_now = size_of.astype(jnp.float32)
        if q < last:
            size_of = prepare(q + 1)
        line = line + build(q)
        line = line + jnp.sum(jnp.where(lane8 == sub8 + (q * TILE + docs), size_now, 0.0), axis=0, keepdims=True)
        if q == 0:
            pl.semaphore_wait(barrier, blocks)
        stage = int(q == last)
        for k in order:
            to = shifted(k)
            remote(outbox.at[q, to], slab.at[grp, q, col], send1.at[stage], recv1.at[stage], (to, grp)).start()
        slab[grp, q, col] = outbox[q, col]
    stat_own[...] = line
    for k in order:
        to = shifted(k)
        remote(stat_own, stat.at[grp, col], send1s.at[0], recv1s.at[0], (to, grp)).start()
    stat[grp, col] = stat_own[...]

    spans = (pl.ds(0, last), pl.ds(last, 1))
    news, hands = [], []
    for stage in range(2):
        came = slab.at[grp, spans[stage], pl.ds(0, peers)]
        news.append(remote(outbox.at[spans[stage], pl.ds(0, peers)], came, send1.at[stage], recv1.at[stage], (col, other)))
        news[stage].wait_recv()
        whole = slab.at[grp, spans[stage]]
        hands.append(remote(whole, whole, send2.at[stage], recv2.at[stage], (col, other)))
        hands[stage].start()

    bw = bw_ref[pl.ds(pl.multiple_of(col * span, span), span)].astype(jnp.float32).reshape(1, span)
    share = blocks // groups
    for stage in range(2):
        hands[stage].wait_recv()
        for q in (range(last), [last])[stage]:
            for o in range(share):
                for g in range(groups):
                    value = slab[g, q, grp * share + o].astype(jnp.float32) * bw
                    weighted[(o * groups + g) * near + q] = value.astype(jnp.bfloat16).astype(jnp.float32)

    def multiply(block):
        tiles = [weighted[cand_ref[0, block, c]] for c in range(picks)]
        lines_in = jnp.concatenate(tiles, axis=0).astype(jnp.bfloat16)
        columns = jnp.concatenate([slab[g, q, block] for g in range(groups) for q in range(near)], axis=0)
        return lax.dot_general(columns, lines_in, NT, preferred_element_type=jnp.float32)

    third = []
    to_zero = lax.bitwise_and(blocks - col, blocks - 1)
    for i, k in enumerate(order):
        if i == 0:
            k = jnp.where(col == 0, k, to_zero)
        else:
            k = jnp.where(to_zero == k, order[0], k)
        block = shifted(k)
        part[k] = multiply(block).astype(part.dtype)
        copy = remote(part.at[k], inbox.at[k], send3.at[k], recv3.at[k], (block, grp))
        copy.start()
        third.append(copy)
    shared = multiply(col)

    news_s = remote(stat.at[grp, pl.ds(0, peers)], stat.at[grp, pl.ds(0, peers)], send1s.at[0], recv1s.at[0], (col, other))
    news_s.wait_recv()
    hand_s = remote(stat.at[grp], stat.at[grp], send2s.at[0], recv2s.at[0], (col, other))
    hand_s.start()
    hand_s.wait_recv()

    pop_rows = jnp.zeros((TILE, LANES), jnp.float32)
    size_rows = jnp.zeros((TILE, LANES), jnp.float32)
    for c in range(picks):
        tile = cand_ref[0, col, c]
        owner = lax.div(tile, near)
        line = stat[lax.rem(owner, groups), grp * share + lax.div(owner, groups)]
        spot = lane8 - lax.rem(tile, near) * TILE - sub8
        pop = jnp.sum(jnp.where(spot == 0, line, 0.0), axis=1, keepdims=True)
        size = jnp.sum(jnp.where(spot == docs, line, 0.0), axis=1, keepdims=True)
        here = lane8 == sub8 + c * TILE
        pop_rows = jnp.where(here, pop, pop_rows)
        size_rows = jnp.where(here, size, size_rows)
    pop_rows = jnp.sum(pop_rows, axis=0, keepdims=True)
    size_rows = jnp.sum(size_rows, axis=0, keepdims=True)
    mine = [stat[g, col] for g in range(groups)]
    pop_cols = jnp.concatenate(
        [jnp.sum(jnp.where(lane == sub, line, 0.0), axis=1, keepdims=True) for line in mine], axis=0)
    size_cols = jnp.concatenate(
        [jnp.sum(jnp.where(lane == sub + docs, line, 0.0), axis=1, keepdims=True) for line in mine], axis=0)

    for k in order[::-1]:
        remote(part.at[k], inbox.at[k], send3.at[k], recv3.at[k], (shifted(k), grp)).wait_recv()
        shared = shared + inbox[k].astype(jnp.float32)
    ratio = shared / (pop_rows + pop_cols - shared)
    out_ref[...] = ratio * (size_rows + size_cols) / ((1.0 + ratio) * jnp.minimum(size_rows, size_cols))
    for copy in third + news + hands + [news_s, hand_s]:
        copy.wait_send()


def fast_body(blocks, groups, positions, element_weights, set_sizes, bit_weights, candidates):
    docs, slots = positions.shape
    span = FILTER_BITS // blocks
    near = docs // TILE
    width, rows = docs * groups, candidates.shape[2] * TILE
    vmem, smem = pl.BlockSpec(memory_space=pltpu.VMEM), pl.BlockSpec(memory_space=pltpu.SMEM)
    sems = pltpu.SemaphoreType.DMA
    scores = pl.pallas_call(
        functools.partial(fused_kernel, blocks, groups),
        out_shape=jax.ShapeDtypeStruct((width, rows), jnp.float32),
        in_specs=[smem, smem, vmem, vmem, vmem],
        out_specs=vmem,
        scratch_shapes=[
            [pltpu.VMEM((4, TILE, slots), jnp.float32) for _ in range(near)],
            [pltpu.VMEM((FILTER_BITS // LANES * TILE, LANES), jnp.float32) for _ in range(near)],
            pltpu.VMEM((near, blocks, TILE, span), jnp.bfloat16),
            pltpu.VMEM((1, LANES), jnp.float32),
            pltpu.VMEM((groups, near, blocks, TILE, span), jnp.bfloat16),
            pltpu.VMEM((groups, blocks, 1, LANES), jnp.float32),
            pltpu.VMEM((docs * blocks // TILE, TILE, span), jnp.float32),
            pltpu.VMEM((blocks, width, rows), jnp.bfloat16),
            pltpu.VMEM((blocks, width, rows), jnp.bfloat16),
            sems((2,)), sems((2,)), sems((1,)), sems((1,)), sems((2,)), sems((2,)), sems((1,)), sems((1,)),
            sems((blocks,)), sems((blocks,)),
        ],
        compiler_params=pltpu.CompilerParams(collective_id=0, has_side_effects=True),
    )(candidates, set_sizes, positions, element_weights, bit_weights)
    return scores.T.reshape(1, 1, rows, width)


def solution(mesh):
    blocks, groups = mesh.shape["bits"], mesh.shape["docs"]
    fits = groups == 2 and FILTER_BITS % (blocks * LANES) == 0
    chosen = functools.partial(fast_body, blocks, groups) if fits else body
    return jax.shard_map(
        chosen,
        mesh=mesh,
        in_specs=(
            P(("bits", "docs"), None),
            P(("bits", "docs"), None),
            P(("bits", "docs")),
            P(),
            P("docs", None, None),
        ),
        out_specs=P("docs", "bits", None, None),
        check_vma=False,
    )
```

time: 33.3 us -> 26 us (0.78)
  the two profiles are of different devices: /device:TPU:0 before, /device:TPU:3 now
where the time goes in v2:
time: 26 us; the launch traced here: 25.8 us
  Pallas kernels  24.5 us (94%)
  local copies, waits for them, and re-layouts  1.38 us (5%)
    pallas_call x1, Pallas kernels, fast_body(): pl.pallas_call(functools.partial(fused_kernel, blocks, groups), out_shape...  24.5 us
    unnamed x1, local copies, waits for them, and re-layouts  1.38 us

profile of v2, /device:TPU:3, one launch (start us, length us, event | category | flops | bytes accessed | tf_op | source)
XLA Modules:
  0.0 25.8 jit_solution(11669333592633256526)
XLA Ops:
  0.0 24.5 %shard_map.55 = f32[64,128]{1,0:T(8,128)} custom-call(s32[1,16,16]{2,1,0:T(8,128)} %cand_ref.1, s32[32]{0:T(128)} %sizes_ref.1, s32[32,4096]{1,0:T(8,128)} %pos_ref.1, f32[32,1024]{1,0:T(8,128)} %elem_ref.1, bf16[4096]{0:T(1024)(128)(2,1)} %bw_ref.1), custom_call_target="tpu_custom_call" | custom-call | tf_op jit(solution)/shard_map/pallas_call | solution.py:332
  24.5 1.4 %copy.7 = f32[1,1,128,64]{2,3,1,0:T(8,128)} copy(f32[1,1,128,64]{2,3,1,0:T(8,128)} %bitcast.3) | data formatting | bytes 65536

commit v3 on v2

--- a/solution.py
+++ b/solution.py
@@ -13,6 +13,7 @@
 TILE = 8
 LANES = 128
 CHUNK = 512
+NEAR_LOW = 4
 STEPS = (0, 127, 126, 3, 122, 6, 125, 8)
 MESH = pl.DeviceIdType.MESH
 
@@ -157,8 +158,12 @@
     lines = FILTER_BITS // LANES
     peers = blocks - 1
 
+    low = min(blocks, NEAR_LOW) - 1
+
     def shifted(k):
-        return lax.bitwise_and(col + k, blocks - 1)
+        k = jnp.int32(k)
+        upper = lax.bitwise_and(lax.bitwise_and(col, blocks - 1 - low) + lax.bitwise_and(k, blocks - 1 - low), blocks - 1)
+        return lax.bitwise_or(upper, lax.bitwise_xor(lax.bitwise_and(col, low), lax.bitwise_and(k, low)))
 
     barrier = pltpu.get_barrier_semaphore()
     for k in range(1, blocks):
@@ -199,7 +204,9 @@
         return pltpu.make_async_remote_copy(
             src_ref=src, dst_ref=dst, send_sem=send, recv_sem=recv, device_id=device, device_id_type=MESH)
 
-    order = sorted(range(1, blocks), key=lambda k: -min(k, blocks - k))
+    steps = blocks // (low + 1)
+    hops = lambda k: min(k // (low + 1), steps - k // (low + 1)) + bin(k & low).count("1")
+    order = sorted(range(1, blocks), key=lambda k: (-hops(k), k))
 
     def build(q):
         for r in range(TILE):
@@ -234,13 +241,16 @@
             size_of = prepare(q + 1)
         line = line + build(q)
         line = line + jnp.sum(jnp.where(lane8 == sub8 + (q * TILE + docs), size_now, 0.0), axis=0, keepdims=True)
+        slab[grp, q, col] = outbox[q, col]
         if q == 0:
+            continue
+        if q == 1:
             pl.semaphore_wait(barrier, blocks)
         stage = int(q == last)
-        for k in order:
-            to = shifted(k)
-            remote(outbox.at[q, to], slab.at[grp, q, col], send1.at[stage], recv1.at[stage], (to, grp)).start()
-        slab[grp, q, col] = outbox[q, col]
+        for s in ((0, 1) if q == 1 else (q,)):
+            for k in order:
+                to = shifted(k)
+                remote(outbox.at[s, to], slab.at[grp, s, col], send1.at[stage], recv1.at[stage], (to, grp)).start()
     stat_own[...] = line
     for k in order:
         to = shifted(k)
@@ -274,7 +284,8 @@
         return lax.dot_general(columns, lines_in, NT, preferred_element_type=jnp.float32)
 
     third = []
-    to_zero = lax.bitwise_and(blocks - col, blocks - 1)
+    to_zero = lax.bitwise_or(lax.bitwise_and(blocks - lax.bitwise_and(col, blocks - 1 - low), blocks - 1),
+                             lax.bitwise_and(col, low))
     for i, k in enumerate(order):
         if i == 0:
             k = jnp.where(col == 0, k, to_zero)
@@ -331,7 +342,7 @@
     sems = pltpu.SemaphoreType.DMA
     scores = pl.pallas_call(
         functools.partial(fused_kernel, blocks, groups),
-        out_shape=jax.ShapeDtypeStruct((width, rows), jnp.float32),
+        out_shape=pltpu.VMEM((width, rows), jnp.float32),
         in_specs=[smem, smem, vmem, vmem, vmem],
         out_specs=vmem,
         scratch_shapes=[

time: 26 us -> 23.6 us (0.908)
  the two profiles are of different devices: /device:TPU:3 before, /device:TPU:9 now
where the time goes in v3:
time: 23.6 us; the launch traced here: 23.5 us
  Pallas kernels  22.8 us (97%)
  local copies, waits for them, and re-layouts  0.62 us (3%)
    pallas_call x1, Pallas kernels, fast_body(): pl.pallas_call(functools.partial(fused_kernel, blocks, groups), out_shape...  22.8 us
    unnamed x1, local copies, waits for them, and re-layouts  0.62 us

profile of v3, /device:TPU:9, one launch (start us, length us, event | category | flops | bytes accessed | tf_op | source)
XLA Modules:
  0.0 23.5 jit_solution(111196009568885085)
XLA Ops:
  0.0 22.8 %shard_map.55 = f32[64,128]{1,0:T(8,128)S(1)} custom-call(s32[1,16,16]{2,1,0:T(8,128)} %cand_ref.1, s32[32]{0:T(128)} %sizes_ref.1, s32[32,4096]{1,0:T(8,128)} %pos_ref.1, f32[32,1024]{1,0:T(8,128)} %elem_ref.1, bf16[4096]{0:T(1024)(128)(2,1)} %bw_ref.1), custom_call_target="tpu_custom_call" | custom-call | tf_op jit(solution)/shard_map/pallas_call | solution.py:343
  22.9 0.6 %copy.7 = f32[1,1,128,64]{2,3,1,0:T(8,128)} copy(f32[1,1,128,64]{2,3,1,0:T(8,128)S(1)} %bitcast.3) | data formatting | bytes 65536

commit v4 on v3

--- a/solution.py
+++ b/solution.py
@@ -286,11 +286,12 @@
     third = []
     to_zero = lax.bitwise_or(lax.bitwise_and(blocks - lax.bitwise_and(col, blocks - 1 - low), blocks - 1),
                              lax.bitwise_and(col, low))
-    for i, k in enumerate(order):
+    late = sorted(order, key=lambda k: (-hops(k), abs(k // (low + 1) - steps // 2), -k))
+    for i, k in enumerate(late):
         if i == 0:
             k = jnp.where(col == 0, k, to_zero)
         else:
-            k = jnp.where(to_zero == k, order[0], k)
+            k = jnp.where(to_zero == k, late[0], k)
         block = shifted(k)
         part[k] = multiply(block).astype(part.dtype)
         copy = remote(part.at[k], inbox.at[k], send3.at[k], recv3.at[k], (block, grp))

time: 23.6 us -> 23.5 us (level)
  the two profiles are of different devices: /device:TPU:9 before, /device:TPU:5 now
where the time goes in v4:
time: 23.5 us; the launch traced here: 23.3 us
  Pallas kernels  22.7 us (97%)
  local copies, waits for them, and re-layouts  0.62 us (3%)
    pallas_call x1, Pallas kernels, fast_body(): pl.pallas_call(functools.partial(fused_kernel, blocks, groups), out_shape...  22.7 us
    unnamed x1, local copies, waits for them, and re-layouts  0.62 us

profile of v4, /device:TPU:5, one launch (start us, length us, event | category | flops | bytes accessed | tf_op | source)
XLA Modules:
  0.0 23.3 jit_solution(6916027094442652862)
XLA Ops:
  0.0 22.7 %shard_map.55 = f32[64,128]{1,0:T(8,128)S(1)} custom-call(s32[1,16,16]{2,1,0:T(8,128)} %cand_ref.1, s32[32]{0:T(128)} %sizes_ref.1, s32[32,4096]{1,0:T(8,128)} %pos_ref.1, f32[32,1024]{1,0:T(8,128)} %elem_ref.1, bf16[4096]{0:T(1024)(128)(2,1)} %bw_ref.1), custom_call_target="tpu_custom_call" | custom-call | tf_op jit(solution)/shard_map/pallas_call | solution.py:344
  22.7 0.6 %copy.7 = f32[1,1,128,64]{2,3,1,0:T(8,128)} copy(f32[1,1,128,64]{2,3,1,0:T(8,128)S(1)} %bitcast.3) | data formatting | bytes 65536
